TPU v7x, 512 devices: a whole 4x4x16 slice. The times are simulated.
512 devices in a mesh: dp: 64 (over z, y_lo, core), tensor: 8 (over x, y_hi).
Axes of the slice: x: 4, y: 4 (y_hi: 2, y_lo: 2; y = y_hi * 2 + y_lo), z: 16, core: 2. Of those that a mesh axis runs over, the one named last changes fastest.
Arguments:
- activations: bfloat16 [131072, 1024], P(('dp', 'tensor')), may hold values from -24 to 24
- gradients: bfloat16 [131072, 5472], P('dp', 'tensor'), may hold values from -6 to 6
- act_history: float32 [8, 16, 1024], P('tensor'), may hold values from 0.1 to 4
- grad_history: float32 [16, 5472], P(None, 'tensor'), may hold values from 0.1 to 4
- owner_rank: int32 [1024], replicated, may hold values from 0 to 7
- history_slot: int32 [6496], replicated, may hold values from 0 to 15
Outputs:
- weight_grad: float32 [1024, 5472], P('dp', 'tensor')
- act_history_out: float32 [8, 16, 1024], P('tensor')
- grad_history_out: float32 [16, 5472], P(None, 'tensor')
All inputs are finite; a program needn't handle non-finite values.
Results may differ from a plain program's by a relative error of at most 0.0042.
Values may be sent and summed in bfloat16 or wider, within the bound.
A program may use at most 64 MiB of HBM per device.

v0:
```python
import math
import jax
import jax.numpy as jnp
from jax import lax
from jax.sharding import PartitionSpec as P

QUANT_LIMIT = 448.0
SCALE_FLOOR = 0.25


def sent_to_all(value, axis):
    copies = jnp.broadcast_to(value, (lax.axis_size(axis), *value.shape))
    return lax.all_to_all(copies, axis, split_axis=0, concat_axis=0, tiled=True)


def of_everyone(value, axis):
    everything = sent_to_all(value, axis)
    return jnp.sum(everything, axis=0)


def cut_along(value, dim, length):
    lengths = value.shape
    parts = value.reshape(*lengths[:dim], length, lengths[dim] // length, *lengths[dim + 1 :])
    return jnp.moveaxis(parts, dim, 0)


def summed_on_arrival(value, axis, dim):
    length = lax.axis_size(axis)
    parts = lax.all_to_all(cut_along(value, dim, length), axis, 0, 0, tiled=True)
    return jnp.sum(parts.astype(jnp.float32), axis=0)


def taken_together(value, axis):
    everything = sent_to_all(value, axis)
    return jnp.max(everything, axis=0)


def in_one(arrays, axis):
    flat, at, done = (jnp.concatenate([a.reshape(-1) for a in arrays]), 0, [])
    subtotal = taken_together(flat, axis)
    for a in arrays:
        done.append(subtotal[at : at + a.size].reshape(a.shape))
        at += a.size
    return tuple(done)


def quantize(values, scale):
    scaled = values.astype(jnp.float32) * scale
    return jnp.clip(scaled, -QUANT_LIMIT, QUANT_LIMIT).astype(jnp.bfloat16)


def place_peaks(history, peaks, slots):
    rows = lax.broadcasted_iota(jnp.int32, history.shape, 0)
    return jnp.where(rows == slots[None, :], peaks[None, :], history)


def body(activations, gradients, act_history, grad_history, owner_rank, history_slot):
    model_width = act_history.shape[2]
    column_total = gradients.shape[1]
    my_rank = lax.axis_index("tensor")
    held = jnp.where(owner_rank[None, :] == my_rank, act_history[0], jnp.float32(0.0))
    current_history = of_everyone(held, "tensor")
    act_scale = QUANT_LIMIT / jnp.maximum(jnp.max(current_history, axis=0), SCALE_FLOOR)
    grad_scale = QUANT_LIMIT / jnp.maximum(jnp.max(grad_history, axis=0), SCALE_FLOOR)
    grad_quant = quantize(gradients, grad_scale)
    row_count = model_width // lax.axis_size("dp")
    grad_factor = 1.0 / math.sqrt(gradients.shape[0] * lax.axis_size("dp"))
    own_grad_peak = jnp.max(jnp.abs(gradients), axis=0).astype(jnp.float32)
    contract_rows = (((0,), (0,)), ((), ()))
    gathered_peak = jnp.zeros((model_width,), jnp.float32)
    act_piece = lax.all_gather(activations, "tensor", axis=0, tiled=True)
    running_peak = gathered_peak
    quantized = quantize(act_piece, act_scale)
    peak_next = jnp.maximum(running_peak, jnp.max(jnp.abs(act_piece), axis=0).astype(jnp.float32))
    partial_sum = lax.dot_general(
        quantized, grad_quant, contract_rows, preferred_element_type=jnp.float32
    )
    partial_sum, gathered_peak = (partial_sum, peak_next)
    summed = summed_on_arrival(partial_sum.astype(jnp.bfloat16), "dp", 0)
    act_peak, grad_peak = in_one((gathered_peak, own_grad_peak), "dp")
    row_base = lax.axis_index("dp") * row_count
    row_scale = lax.dynamic_slice_in_dim(act_scale, row_base, row_count, 0)
    weight_grad = summed / (row_scale[:, None] * grad_scale[None, :]) * grad_factor
    act_slots = history_slot[:model_width]
    grad_slots = lax.dynamic_slice_in_dim(
        history_slot, model_width + my_rank * column_total, column_total, 0
    )
    updated = place_peaks(current_history, act_peak, act_slots)
    act_history_out = updated[None]
    grad_history_out = place_peaks(grad_history, grad_peak, grad_slots)
    return (weight_grad, act_history_out, grad_history_out)


def solution(mesh):
    placed = (
        P(("dp", "tensor"), None),
        P("dp", "tensor"),
        P("tensor", None, None),
        P(None, "tensor"),
        P(),
        P(),
    )
    return jax.shard_map(
        body,
        mesh=mesh,
        in_specs=placed,
        out_specs=(P("dp", "tensor"), P("tensor", None, None), P(None, "tensor")),
        check_vma=False,
    )
```

profile of v0, /device:TPU:8, one launch (start us, length us, event | category | flops | bytes accessed | tf_op | source)
XLA Modules:
  0.0 252.6 jit_solution(7629873349470279669)
XLA Ops:
  7.2 0.0 all-gather.2.cloned.1.call-start
  7.2 0.7 all-gather.2.cloned.1.call-update
  7.9 0.7 broadcast_compare_fusion
  8.6 0.8 bitcast_select_fusion.1
  9.4 0.8 broadcast_in_dim.49
  10.3 6.0 %all-to-all-start = ((f32[8,16,1024]{2,1,0:T(8,128)}), f32[8,16,1024]{2,1,0:T(8,128)S(1)}, u32[]{:S(2)}, u32[]{:S(2)}) async-start(f32[8,16,1024]{2,1,0:T(8,128)} %broadcast_in_dim.49), calls=%async_computation | async-start | bytes 1048576 | tf_op jit(solution)/shard_map/all_to_all | solution.py:13
  16.3 0.0 copy-start.2
  16.3 0.0 copy-start.1
  16.3 0.0 copy-start
  16.3 2.6 %abs_reduce_fusion.1 = bf16[684]{0:T(1024)(128)(2,1)S(1)} fusion(bf16[2048,684]{0,1:T(8,128)(2,1)} %param.7), kind=kLoop, calls=%fused_computation.8 | loop fusion | flops 2800980 | bytes 2803032 | tf_op jit(solution)/shard_map/reduce_max | solution.py:68
  18.9 82.8 %all-gather.2.cloned.1.call-done = bf16[2048,1024]{1,0:T(8,128)(2,1)} async-done(((bf16[256,1024]{1,0:T(8,128)(2,1)}), bf16[2048,1024]{1,0:T(8,128)(2,1)}) %all-gather.2.cloned.1.call-update) | async-done | bytes 4194320 | tf_op jit(solution)/shard_map/all_gather | solution.py:71
  101.7 2.6 %abs_reduce_fusion = bf16[1024]{0:T(1024)(128)(2,1)S(1)} fusion(bf16[2048,1024]{1,0:T(8,128)(2,1)} %all-gather.2.cloned.1.call-done), kind=kLoop, calls=%fused_computation.3 | loop fusion | flops 4193280 | bytes 4196352 | tf_op jit(solution)/shard_map/reduce_max | solution.py:74
  104.3 0.0 all-to-all-done
  104.4 1.0 broadcast_in_dim.51
  105.4 14.4 %all-to-all-start.2 = ((f32[64,1,1708]{2,1,0:T(1,128)}), f32[64,1,1708]{2,1,0:T(1,128)}, u32[]{:S(2)}, u32[]{:S(2)}) async-start(f32[64,1,1708]{2,1,0:T(1,128)} %broadcast_in_dim.51), calls=%async_computation.2 | async-start | bytes 917504 | tf_op jit(solution)/shard_map/all_to_all | solution.py:13
  119.8 0.0 copy-done.2
  119.8 0.1 dynamic_slice.7
  119.9 30.5 %all-to-all-done.2 = f32[64,1,1708]{2,1,0:T(1,128)} async-done(((f32[64,1,1708]{2,1,0:T(1,128)}), f32[64,1,1708]{2,1,0:T(1,128)}, u32[]{:S(2)}, u32[]{:S(2)}) %all-to-all-start.2) | async-done | bytes 437280 | tf_op jit(solution)/shard_map/all_to_all | solution.py:13
  150.4 1.3 reduce_max.49
  151.8 0.0 copy-done.1
  151.8 0.6 fusion.8
  152.4 0.0 copy-done
  152.4 6.5 %fusion.7 = bf16[1024,684]{0,1:T(8,128)(2,1)} fusion(bf16[2048,684]{0,1:T(8,128)(2,1)S(1)} %copy-done, f32[684]{0:T(1024)S(1)} %maximum_divide_fusion, bf16[2048,1024]{1,0:T(8,128)(2,1)} %all-gather.2.cloned.1.call-done, f32[1024]{0:T(1024)S(1)} %maximum_divide_fusion.1), kind=kOutput, calls=%fused_computation.12 | convolution fusion | flops 2883596288 | bytes 8403632 | tf_op jit(solution)/shard_map/dot_general | solution.py:75
  158.9 0.0 slice-start
  158.9 2.6 %copy.11 = bf16[1024,684]{1,0:T(8,128)(2,1)} copy(bf16[1024,684]{0,1:T(8,128)(2,1)} %fusion.7) | data formatting | bytes 2801664 | tf_op jit(solution)/shard_map/convert_element_type | solution.py:79
  161.5 4.7 %all-to-all-start.1 = ((bf16[64,16,684]{2,1,0:T(8,128)(2,1)}), bf16[64,16,684]{2,1,0:T(8,128)(2,1)S(1)}, u32[]{:S(2)}, u32[]{:S(2)}) async-start(bf16[64,16,684]{2,1,0:T(8,128)(2,1)} %bitcast.1), calls=%async_computation.1 | async-start | bytes 3145728 | tf_op jit(solution)/shard_map/all_to_all | solution.py:29
  166.2 0.1 dynamic_slice.6
  166.3 0.0 slice-done
  166.3 0.6 bitcast_select_fusion
  166.9 77.9 %all-to-all-done.1 = bf16[64,16,684]{2,1,0:T(8,128)(2,1)S(1)} async-done(((bf16[64,16,684]{2,1,0:T(8,128)(2,1)}), bf16[64,16,684]{2,1,0:T(8,128)(2,1)S(1)}, u32[]{:S(2)}, u32[]{:S(2)}) %all-to-all-start.1) | async-done | bytes 1400864 | tf_op jit(solution)/shard_map/all_to_all | solution.py:29
  244.8 0.3 convert_reduce_fusion
  245.1 0.7 divide_multiply_fusion
  (9 shorter events, 0.1 us)
Async XLA Ops:
  7.2 94.5 %all-gather.2.cloned.1.call-start = ((), (), s32[]{:S(2)}) async-start(), calls=%async_computation.3 | async-start | bytes 4718592 | tf_op jit(solution)/shard_map/all_gather | solution.py:71
  10.3 94.1 %all-to-all-start = ((f32[8,16,1024]{2,1,0:T(8,128)}), f32[8,16,1024]{2,1,0:T(8,128)S(1)}, u32[]{:S(2)}, u32[]{:S(2)}) async-start(f32[8,16,1024]{2,1,0:T(8,128)} %broadcast_in_dim.49), calls=%async_computation | async-start | bytes 1048576 | tf_op jit(solution)/shard_map/all_to_all | solution.py:13
  16.3 103.4 %copy-start.2 = (s32[6496]{0:T(1024)S(1)}, s32[6496]{0:T(1024)}, u32[]{:S(2)}) copy-start(s32[6496]{0:T(1024)} %param.11) | copy-start | bytes 77956
  16.3 135.4 %copy-start.1 = (f32[16,684]{1,0:T(8,128)S(1)}, f32[16,684]{1,0:T(8,128)}, u32[]{:S(2)}) copy-start(f32[16,684]{1,0:T(8,128)} %param.9) | copy-start | bytes 131332
  16.3 136.1 %copy-start = (bf16[2048,684]{0,1:T(8,128)(2,1)S(1)}, bf16[2048,684]{0,1:T(8,128)(2,1)}, u32[]{:S(2)}) copy-start(bf16[2048,684]{0,1:T(8,128)(2,1)} %param.7) | copy-start | bytes 8404996
  105.4 45.1 %all-to-all-start.2 = ((f32[64,1,1708]{2,1,0:T(1,128)}), f32[64,1,1708]{2,1,0:T(1,128)}, u32[]{:S(2)}, u32[]{:S(2)}) async-start(f32[64,1,1708]{2,1,0:T(1,128)} %broadcast_in_dim.51), calls=%async_computation.2 | async-start | bytes 917504 | tf_op jit(solution)/shard_map/all_to_all | solution.py:13
  158.9 7.4 %slice-start = ((s32[6496]{0:T(1024)}), s32[1024]{0:T(1024)S(1)}, s32[]{:S(2)}) async-start(s32[6496]{0:T(1024)} %param.11), calls=%async_computation.4 | async-start | bytes 8192 | tf_op jit(solution)/shard_map/slice | solution.py:84
  161.5 83.3 %all-to-all-start.1 = ((bf16[64,16,684]{2,1,0:T(8,128)(2,1)}), bf16[64,16,684]{2,1,0:T(8,128)(2,1)S(1)}, u32[]{:S(2)}, u32[]{:S(2)}) async-start(bf16[64,16,684]{2,1,0:T(8,128)(2,1)} %bitcast.1), calls=%async_computation.1 | async-start | bytes 3145728 | tf_op jit(solution)/shard_map/all_to_all | solution.py:29
Sparse Core Ops, SparseCore 0:
  11.2 90.4 all-gather.1
where the time goes:
time: 253 us
  waiting for transfers between devices  192 us (76%)
  starting transfers between devices  25.1 us (10%)
  between operations  14.1 us (6%)
  other arithmetic  10.3 us (4%)
  matrix products  6.51 us (3%)
  local copies, waits for them, and re-layouts  4.63 us (2%)
    all_gather x1, waiting for transfers between devices, body(): act_piece = lax.all_gather(activations, 'tensor', axis=0, tiled=True)  82.8 us
    all_to_all x1, waiting for transfers between devices, summed_on_arrival(): lax.all_to_all(cut_along(value, dim, length), axis, 0, 0, tiled=True)  77.9 us
    all_to_all x2, waiting for transfers between devices, sent_to_all(): return lax.all_to_all(copies, axis, split_axis=0, concat_axis=0, tiled=True)  30.5 us
    all_to_all x2, starting transfers between devices, sent_to_all(): return lax.all_to_all(copies, axis, split_axis=0, concat_axis=0, tiled=True)  20.4 us
    dot_general x1, matrix products, body(): lax.dot_general(quantized, grad_quant, contract_rows, preferred_element_t...  6.51 us
  transfers between devices with their start and end apart: 4, of which 3 were waited for; matrix products, arithmetic and copies ran while one was open for 3% of the time, Pallas kernels for 0%

commit v1 on v0

--- a/solution.py
+++ b/solution.py
@@ -68,7 +68,9 @@
     own_grad_peak = jnp.max(jnp.abs(gradients), axis=0).astype(jnp.float32)
     contract_rows = (((0,), (0,)), ((), ()))
     gathered_peak = jnp.zeros((model_width,), jnp.float32)
-    act_piece = lax.all_gather(activations, "tensor", axis=0, tiled=True)
+    act_piece = jnp.concatenate(
+        lax.all_to_all(jnp.stack([activations] * lax.axis_size("tensor")), "tensor", 0, 0), axis=0
+    )
     running_peak = gathered_peak
     quantized = quantize(act_piece, act_scale)
     peak_next = jnp.maximum(running_peak, jnp.max(jnp.abs(act_piece), axis=0).astype(jnp.float32))

time: 253 us -> 231 us (0.913)
  waiting for transfers between devices: 192 us -> 175 us
  between operations: 14.1 us -> 0.76 us
  starting transfers between devices: 25.1 us -> 33.3 us
  local copies, waits for them, and re-layouts: 4.63 us -> 8.19 us
  other arithmetic: 10.3 us -> 6.86 us
    all_gather x1 -> x0, waiting for transfers between devices: 82.8 us -> none  [body(): act_piece = lax.all_gather(activations, 'tensor', axis=0, tiled=True)]
    all_to_all x0 -> x1, waiting for transfers between devices: none -> 58.9 us  [body(): lax.all_to_all(jnp.stack([activations] * lax.axis_size('tensor')), 'tenso...]
    all_to_all x2, waiting for transfers between devices: 30.5 us -> 38 us  [sent_to_all(): return lax.all_to_all(copies, axis, split_axis=0, concat_axis=0, tiled=True)]
    all_to_all x0 -> x1, starting transfers between devices: none -> 6.29 us  [body(): lax.all_to_all(jnp.stack([activations] * lax.axis_size('tensor')), 'tenso...]
    another operation x0 -> x1, local copies, waits for them, and re-layouts: none -> 3.55 us  [body(): jnp.stack([activations] * lax.axis_size('tensor'))]
  transfers between devices with their start and end apart: 4 -> 4, of which waited for: 3 -> 4; matrix products, arithmetic and copies ran while one was open for 3% -> 2% of each run, Pallas kernels for 0% -> 0%
where the time goes in v1:
time: 231 us; the launch traced here: 230 us
  waiting for transfers between devices  175 us (76%)
  starting transfers between devices  33.3 us (14%)
  local copies, waits for them, and re-layouts  8.19 us (4%)
  other arithmetic  6.86 us (3%)
  matrix products  6.5 us (3%)
    all_to_all x1, waiting for transfers between devices, summed_on_arrival(): lax.all_to_all(cut_along(value, dim, length), axis, 0, 0, tiled=True)  77.9 us
    all_to_all x1, waiting for transfers between devices, body(): lax.all_to_all(jnp.stack([activations] * lax.axis_size('tensor')), 'tenso...  58.9 us
    all_to_all x2, waiting for transfers between devices, sent_to_all(): return lax.all_to_all(copies, axis, split_axis=0, concat_axis=0, tiled=True)  38 us
    all_to_all x2, starting transfers between devices, sent_to_all(): return lax.all_to_all(copies, axis, split_axis=0, concat_axis=0, tiled=True)  22.3 us
    dot_general x1, matrix products, body(): lax.dot_general(quantized, grad_quant, contract_rows, preferred_element_t...  6.5 us
    all_to_all x1, starting transfers between devices, body(): lax.all_to_all(jnp.stack([activations] * lax.axis_size('tensor')), 'tenso...  6.29 us
    all_to_all x1, starting transfers between devices, summed_on_arrival(): lax.all_to_all(cut_along(value, dim, length), axis, 0, 0, tiled=True)  4.69 us
  transfers between devices with their start and end apart: 4, of which 4 were waited for; matrix products, arithmetic and copies ran while one was open for 2% of the time, Pallas kernels for 0%

profile of v1, /device:TPU:8, one launch (start us, length us, event | category | flops | bytes accessed | tf_op | source)
XLA Modules:
  0.0 230.4 jit_solution(12907136774859733343)
XLA Ops:
  0.6 3.5 %stack.2 = bf16[8,256,1024]{2,1,0:T(8,128)(2,1)} broadcast(bf16[256,1024]{1,0:T(8,128)(2,1)} %param.6), dimensions={1,2} | broadcast | bytes 4718592 | tf_op jit(solution)/shard_map/stack | solution.py:72
  4.2 0.0 copy-start
  4.2 0.0 copy-start.4
  4.2 0.0 copy-start.1
  4.2 6.3 %all-to-all-start = ((bf16[8,256,1024]{2,1,0:T(8,128)(2,1)}), bf16[8,256,1024]{2,1,0:T(8,128)(2,1)}, u32[]{:S(2)}, u32[]{:S(2)}) async-start(bf16[8,256,1024]{2,1,0:T(8,128)(2,1)} %stack.2), calls=%async_computation | async-start | bytes 8388608 | tf_op jit(solution)/shard_map/all_to_all | solution.py:72
  10.5 0.0 copy-done
  10.5 0.6 abs_reduce_fusion.1
  11.1 0.0 copy-start.3
  11.1 0.0 copy-done.4
  11.1 0.0 copy-done.1
  11.2 0.0 copy-start.2
  11.2 58.9 %all-to-all-done = bf16[8,256,1024]{2,1,0:T(8,128)(2,1)} async-done(((bf16[8,256,1024]{2,1,0:T(8,128)(2,1)}), bf16[8,256,1024]{2,1,0:T(8,128)(2,1)}, u32[]{:S(2)}, u32[]{:S(2)}) %all-to-all-start) | async-done | bytes 4194336 | tf_op jit(solution)/shard_map/all_to_all | solution.py:72
  70.1 0.8 broadcast_in_dim.49
  70.9 5.0 %all-to-all-start.1 = ((f32[8,16,1024]{2,1,0:T(8,128)}), f32[8,16,1024]{2,1,0:T(8,128)S(1)}, u32[]{:S(2)}, u32[]{:S(2)}) async-start(f32[8,16,1024]{2,1,0:T(8,128)} %broadcast_in_dim.49), calls=%async_computation.1 | async-start | bytes 1048576 | tf_op jit(solution)/shard_map/all_to_all | solution.py:13
  76.0 2.6 %abs_reduce_fusion = bf16[1024]{0:T(1024)(128)(2,1)S(1)} fusion(bf16[8,256,1024]{2,1,0:T(8,128)(2,1)} %all-to-all-done), kind=kLoop, calls=%fused_computation.5 | loop fusion | flops 4193280 | bytes 4196352 | tf_op jit(solution)/shard_map/reduce_max | solution.py:76
  78.6 7.4 %all-to-all-done.1 = f32[8,16,1024]{2,1,0:T(8,128)S(1)} async-done(((f32[8,16,1024]{2,1,0:T(8,128)}), f32[8,16,1024]{2,1,0:T(8,128)S(1)}, u32[]{:S(2)}, u32[]{:S(2)}) %all-to-all-start.1) | async-done | bytes 524320 | tf_op jit(solution)/shard_map/all_to_all | solution.py:13
  86.0 1.0 broadcast_in_dim.51
  87.1 17.3 %all-to-all-start.3 = ((f32[64,1,1708]{2,1,0:T(1,128)}), f32[64,1,1708]{2,1,0:T(1,128)}, u32[]{:S(2)}, u32[]{:S(2)}) async-start(f32[64,1,1708]{2,1,0:T(1,128)} %broadcast_in_dim.51), calls=%async_computation.3 | async-start | bytes 917504 | tf_op jit(solution)/shard_map/all_to_all | solution.py:13
  104.4 0.0 copy-done.3
  104.4 0.1 dynamic_slice.7
  104.5 30.5 %all-to-all-done.3 = f32[64,1,1708]{2,1,0:T(1,128)} async-done(((f32[64,1,1708]{2,1,0:T(1,128)}), f32[64,1,1708]{2,1,0:T(1,128)}, u32[]{:S(2)}, u32[]{:S(2)}) %all-to-all-start.3) | async-done | bytes 437280 | tf_op jit(solution)/shard_map/all_to_all | solution.py:13
  135.0 1.3 reduce_max.49
  136.3 0.0 copy-done.2
  136.4 0.6 fusion.13
  137.0 6.5 %fusion.10 = bf16[1024,684]{0,1:T(8,128)(2,1)} fusion(bf16[2048,684]{0,1:T(8,128)(2,1)S(1)} %copy-done, f32[684]{0:T(1024)S(1)} %maximum_divide_fusion, bf16[2048,1024]{1,0:T(8,128)(2,1)} %bitcast.4, f32[1024]{0:T(1024)S(1)} %maximum_divide_fusion.1), kind=kOutput, calls=%fused_computation.14 | convolution fusion | flops 2883596288 | bytes 8403632 | tf_op jit(solution)/shard_map/dot_general | solution.py:77
  143.5 0.0 slice-start
  143.5 2.6 %copy.11 = bf16[1024,684]{1,0:T(8,128)(2,1)} copy(bf16[1024,684]{0,1:T(8,128)(2,1)} %fusion.10) | data formatting | bytes 2801664 | tf_op jit(solution)/shard_map/convert_element_type | solution.py:81
  146.1 4.7 %all-to-all-start.2 = ((bf16[64,16,684]{2,1,0:T(8,128)(2,1)}), bf16[64,16,684]{2,1,0:T(8,128)(2,1)S(1)}, u32[]{:S(2)}, u32[]{:S(2)}) async-start(bf16[64,16,684]{2,1,0:T(8,128)(2,1)} %bitcast.2), calls=%async_computation.2 | async-start | bytes 3145728 | tf_op jit(solution)/shard_map/all_to_all | solution.py:29
  150.8 0.1 dynamic_slice.6
  150.9 0.0 slice-done
  150.9 0.6 bitcast_select_fusion
  151.5 77.9 %all-to-all-done.2 = bf16[64,16,684]{2,1,0:T(8,128)(2,1)S(1)} async-done(((bf16[64,16,684]{2,1,0:T(8,128)(2,1)}), bf16[64,16,684]{2,1,0:T(8,128)(2,1)S(1)}, u32[]{:S(2)}, u32[]{:S(2)}) %all-to-all-start.2) | async-done | bytes 1400864 | tf_op jit(solution)/shard_map/all_to_all | solution.py:29
  229.4 0.3 convert_reduce_fusion
  229.7 0.7 divide_multiply_fusion
  (11 shorter events, 0.1 us)
Async XLA Ops:
  4.2 6.3 %copy-start = (bf16[2048,684]{0,1:T(8,128)(2,1)S(1)}, bf16[2048,684]{0,1:T(8,128)(2,1)}, u32[]{:S(2)}) copy-start(bf16[2048,684]{0,1:T(8,128)(2,1)} %param.7) | copy-start | bytes 8404996
  4.2 6.9 %copy-start.4 = (s32[1024]{0:T(1024)S(1)}, s32[1024]{0:T(1024)}, u32[]{:S(2)}) copy-start(s32[1024]{0:T(1024)} %param.10) | copy-start | bytes 12292
  4.2 7.0 %copy-start.1 = (f32[1,16,1024]{2,1,0:T(8,128)S(1)}, f32[1,16,1024]{2,1,0:T(8,128)}, u32[]{:S(2)}) copy-start(f32[1,16,1024]{2,1,0:T(8,128)} %param.8) | copy-start | bytes 196612
  4.2 65.9 %all-to-all-start = ((bf16[8,256,1024]{2,1,0:T(8,128)(2,1)}), bf16[8,256,1024]{2,1,0:T(8,128)(2,1)}, u32[]{:S(2)}, u32[]{:S(2)}) async-start(bf16[8,256,1024]{2,1,0:T(8,128)(2,1)} %stack.2), calls=%async_computation | async-start | bytes 8388608 | tf_op jit(solution)/shard_map/all_to_all | solution.py:72
  11.1 93.3 %copy-start.3 = (s32[6496]{0:T(1024)S(1)}, s32[6496]{0:T(1024)}, u32[]{:S(2)}) copy-start(s32[6496]{0:T(1024)} %param.11) | copy-start | bytes 77956
  11.2 125.2 %copy-start.2 = (f32[16,684]{1,0:T(8,128)S(1)}, f32[16,684]{1,0:T(8,128)}, u32[]{:S(2)}) copy-start(f32[16,684]{1,0:T(8,128)} %param.9) | copy-start | bytes 131332
  70.9 15.1 %all-to-all-start.1 = ((f32[8,16,1024]{2,1,0:T(8,128)}), f32[8,16,1024]{2,1,0:T(8,128)S(1)}, u32[]{:S(2)}, u32[]{:S(2)}) async-start(f32[8,16,1024]{2,1,0:T(8,128)} %broadcast_in_dim.49), calls=%async_computation.1 | async-start | bytes 1048576 | tf_op jit(solution)/shard_map/all_to_all | solution.py:13
  87.1 48.0 %all-to-all-start.3 = ((f32[64,1,1708]{2,1,0:T(1,128)}), f32[64,1,1708]{2,1,0:T(1,128)}, u32[]{:S(2)}, u32[]{:S(2)}) async-start(f32[64,1,1708]{2,1,0:T(1,128)} %broadcast_in_dim.51), calls=%async_computation.3 | async-start | bytes 917504 | tf_op jit(solution)/shard_map/all_to_all | solution.py:13
  143.5 7.4 %slice-start = ((s32[6496]{0:T(1024)}), s32[1024]{0:T(1024)S(1)}, s32[]{:S(2)}) async-start(s32[6496]{0:T(1024)} %param.11), calls=%async_computation.4 | async-start | bytes 8192 | tf_op jit(solution)/shard_map/slice | solution.py:86
  146.1 83.3 %all-to-all-start.2 = ((bf16[64,16,684]{2,1,0:T(8,128)(2,1)}), bf16[64,16,684]{2,1,0:T(8,128)(2,1)S(1)}, u32[]{:S(2)}, u32[]{:S(2)}) async-start(bf16[64,16,684]{2,1,0:T(8,128)(2,1)} %bitcast.2), calls=%async_computation.2 | async-start | bytes 3145728 | tf_op jit(solution)/shard_map/all_to_all | solution.py:29
